TPU v7x, 512 devices: a whole 4x8x8 slice. The times are simulated.
512 devices in a mesh: grp: 16 (over y, x_lo), row: 8 (over z), col: 4 (over x_hi, core).
Axes of the slice: x: 4 (x_hi: 2, x_lo: 2; x = x_hi * 2 + x_lo), y: 8, z: 8, core: 2. Of those that a mesh axis runs over, the one named last changes fastest.
Arguments:
- normals: float32 [16, 4096, 4096], P('grp', 'row', 'col'), as said below
- transforms: float32 [16, 32, 128, 128], P('grp', 'row'), as said below
- block_map: int32 [16, 32], P('grp'), may hold values from 0 to 31, as said below
Outputs:
- eliminated: float32 [4096, 4096], P('row', 'col')
Inputs may be any that keep to these rules, and one draw needn't show every extreme that they name: `block_map`: for each group, a permutation of the blocks that maps every aligned range of 4 blocks onto itself. `normals`: each group's matrix is symmetric positive definite. `transforms`: each block is nonsingular.
All inputs are finite; a program needn't handle non-finite values.
Results may differ from a plain program's by a relative error of at most 0.0001.
Values sent between devices are 32-bit elements; how exact they have to be, the bound alone decides.
A program may use at most 64 MiB of HBM per device.

v0:
```python
import jax
import jax.numpy as jnp
from jax import lax
from jax.sharding import PartitionSpec as P

BLK = 128
NPAN = 5


def split_up(shard, dim, length):
    shape = shard.shape
    parts = shard.reshape(*shape[:dim], length, shape[dim] // length, *shape[dim + 1 :])
    return jnp.moveaxis(parts, dim, 0)


def sum_at_owner(shard, axis, dim):
    parts = split_up(shard, dim, lax.axis_size(axis))
    arrived = lax.all_to_all(parts, axis, split_axis=0, concat_axis=0, tiled=True)
    return arrived.sum(axis=0)


def from_root(shard, axis, root):
    return lax.dynamic_index_in_dim(lax.all_gather(shard, axis), root, 0, keepdims=False)


def in_order(parts, dim):
    parts = jnp.moveaxis(parts, 0, dim)
    shape = parts.shape
    return parts.reshape(*shape[:dim], shape[dim] * shape[dim + 1], *shape[dim + 2 :])


def sent_to_all(shard, axis):
    length = lax.axis_size(axis)
    return lax.all_to_all(
        jnp.broadcast_to(shard[None], (length, *shard.shape)), axis, 0, 0, tiled=True
    )


def gather_directly(shard, axis, dim):
    return in_order(sent_to_all(shard, axis), dim)


def on_device(normals, transforms, block_map):
    local = normals[0]
    height, width = local.shape
    row_blocks = height // BLK
    col_blocks = width // BLK
    row_index = lax.axis_index("row")
    col_index = lax.axis_index("col")
    row_transforms = transforms[0]
    every_block = lax.all_gather(transforms, "row", axis=1, tiled=True)[0]
    col_transforms = lax.dynamic_slice_in_dim(every_block, col_index * col_blocks, col_blocks, 0)
    grid = local.reshape(row_blocks, BLK, col_blocks, BLK)
    half_done = jnp.einsum("aij,aibk->ajbk", row_transforms, grid, precision=lax.Precision.HIGHEST)
    rotated = jnp.einsum(
        "ajbk,bkl->ajbl", half_done, col_transforms, precision=lax.Precision.HIGHEST
    )
    mapping = block_map[0]
    row_map = (
        lax.dynamic_slice_in_dim(mapping, row_index * row_blocks, row_blocks, 0)
        - row_index * row_blocks
    )
    col_map = (
        lax.dynamic_slice_in_dim(mapping, col_index * col_blocks, col_blocks, 0)
        - col_index * col_blocks
    )
    rotated = jnp.take(rotated, row_map, axis=0)
    rotated = jnp.take(rotated, col_map, axis=2).reshape(height, width)
    matrix = sum_at_owner(rotated, "grp", 0)
    row_offset = row_index * height + lax.axis_index("grp") * matrix.shape[0]
    own_count = matrix.shape[0]
    order_all = height * lax.axis_size("row")
    col_offset = col_index * width
    for panel in range(NPAN):
        offset = panel * BLK
        holder = offset // width
        inside = offset - holder * width
        panel_piece = from_root(matrix[:, inside : inside + BLK], "col", holder)
        panel_piece = gather_directly(panel_piece, "grp", 0)
        column = lax.all_gather(panel_piece, "row", axis=0, tiled=True)
        factor_block = jnp.linalg.cholesky(column[offset : offset + BLK])
        factor = lax.linalg.triangular_solve(
            factor_block, column, left_side=False, lower=True, transpose_a=True
        )
        below = jnp.arange(order_all)[:, None] >= offset
        factor = jnp.where(below, factor, jnp.zeros_like(factor))
        own_rows = lax.dynamic_slice_in_dim(factor, row_offset, own_count, 0)
        col_rows = lax.dynamic_slice_in_dim(factor, col_offset, width, 0)
        matrix = matrix - jnp.dot(
            own_rows,
            col_rows.T,
            precision=lax.Precision.HIGHEST,
            preferred_element_type=jnp.float32,
        )
        current = matrix[:, inside : inside + BLK]
        matrix = matrix.at[:, inside : inside + BLK].set(
            jnp.where(col_index == holder, own_rows, current)
        )
    matrix = gather_directly(matrix, "grp", 0)
    return matrix


def solution(mesh):
    return jax.shard_map(
        on_device,
        mesh=mesh,
        in_specs=(P("grp", "row", "col"), P("grp", "row", None, None), P("grp", None)),
        out_specs=P("row", "col"),
        check_vma=False,
    )
```

profile of v0, /device:TPU:4, one launch (start us, length us, event | category | flops | bytes accessed | tf_op | source)
XLA Modules:
  0.0 668.6 jit_solution(9049926611283162796)
XLA Ops:
  7.3 3.4 copy.93
  11.2 3.7 fusion.4
  14.9 43.2 %all-gather.12.cloned.1.call-done = f32[1,32,128,128]{3,2,0,1:T(8,128)} async-done(((f32[1,4,128,128]{3,2,0,1:T(8,128)}), f32[1,32,128,128]{3,2,0,1:T(8,128)}) %all-gather.12.cloned.1.call-update) | async-done | bytes 2097168 | tf_op jit(solution)/shard_map/all_gather | solution.py:51
  58.0 4.3 convolution_bitcast_fusion.5
  62.3 2.3 gather_fusion
  64.6 1.6 broadcast_select_fusion.1
  66.2 2.3 gather_fusion.1
  68.5 1.8 copy.69
  70.3 1.7 gather.12
  72.3 54.1 %all_to_all.35 = f32[16,32,1024]{2,1,0:T(8,128)S(1)} all-to-all(f32[16,32,1024]{2,1,0:T(8,128)S(1)} %broadcast_select_fusion), channel_id=1, replica_groups=mesh['grp'=16,'row'=8,'col'=4] {'grp'}, dimensions={0} | all-to-all | bytes 4194304 | tf_op jit(solution)/shard_map/all_to_all | solution.py:18
  126.5 6.7 %all-gather = f32[128,128]{1,0:T(8,128)S(1)} all-gather(f32[32,128]{1,0:T(8,128)S(1)} %slice.165), channel_id=2, replica_groups=mesh['grp'=16,'row'=8,'col'=4] {'col'}, dimensions={0}, use_global_device_ids=true | all-gather | bytes 81920 | tf_op jit(solution)/shard_map/all_gather | solution.py:23
  133.3 15.9 %all_to_all.36 = f32[16,32,128]{2,1,0:T(8,128)S(1)} all-to-all(f32[16,32,128]{2,1,0:T(8,128)S(1)} %broadcast_in_dim.111), channel_id=1, replica_groups=mesh['grp'=16,'row'=8,'col'=4] {'grp'}, dimensions={0} | all-to-all | bytes 524288 | tf_op jit(solution)/shard_map/all_to_all | solution.py:34
  150.9 36.5 %all-gather.14.cloned.1.call-done = f32[4096,128]{0,1:T(8,128)} async-done(((f32[512,128]{0,1:T(8,128)}), f32[4096,128]{0,1:T(8,128)}) %all-gather.14.cloned.1.call-update) | async-done | bytes 2097168 | tf_op jit(solution)/shard_map/all_gather | solution.py:80
  187.3 0.8 slice.167
  188.3 0.9 fusion.28
  189.1 11.7 %cholesky.89 = f32[128,128]{1,0:T(8,128)S(1)} custom-call(f32[128,128]{1,0:T(8,128)S(1)} %fusion.28), custom_call_target="Cholesky" | custom-call | tf_op jit(solution)/shard_map/jit(cholesky)/cholesky | solution.py:81
  202.2 9.8 %custom-call.9 = f32[1,128,128]{1,2,0:T(8,128)S(1)} custom-call(f32[1,128,128]{2,1,0:T(8,128)S(1)} %fusion.14), custom_call_target="InvertDiagBlocksLowerTriangular" | custom-call | tf_op jit(solution)/shard_map/triangular_solve/custom-call.0 | solution.py:82
  212.0 5.1 convolution_bitcast_fusion.4
  218.4 6.7 %all-gather.1 = f32[128,128]{1,0:T(8,128)S(1)} all-gather(f32[32,128]{1,0:T(8,128)S(1)} %slice.169), channel_id=3, replica_groups=mesh['grp'=16,'row'=8,'col'=4] {'col'}, dimensions={0}, use_global_device_ids=true | all-gather | bytes 81920 | tf_op jit(solution)/shard_map/all_gather | solution.py:23
  225.2 19.7 %all_to_all.37 = f32[16,32,128]{2,1,0:T(8,128)S(1)} all-to-all(f32[16,32,128]{2,1,0:T(8,128)S(1)} %broadcast_in_dim.114), channel_id=1, replica_groups=mesh['grp'=16,'row'=8,'col'=4] {'grp'}, dimensions={0} | all-to-all | bytes 524288 | tf_op jit(solution)/shard_map/all_to_all | solution.py:34
  246.7 37.3 %all-gather.16.cloned.1.call-done = f32[4096,128]{0,1:T(8,128)} async-done(((f32[512,128]{0,1:T(8,128)}), f32[4096,128]{0,1:T(8,128)}) %all-gather.16.cloned.1.call-update) | async-done | bytes 2097168 | tf_op jit(solution)/shard_map/all_gather | solution.py:80
  284.9 0.9 fusion.26
  285.8 11.7 %cholesky.100 = f32[128,128]{1,0:T(8,128)S(1)} custom-call(f32[128,128]{1,0:T(8,128)S(1)} %fusion.26), custom_call_target="Cholesky" | custom-call | tf_op jit(solution)/shard_map/jit(cholesky)/cholesky | solution.py:81
  298.8 9.8 %custom-call.10 = f32[1,128,128]{1,2,0:T(8,128)S(1)} custom-call(f32[1,128,128]{2,1,0:T(8,128)S(1)} %fusion.15), custom_call_target="InvertDiagBlocksLowerTriangular" | custom-call | tf_op jit(solution)/shard_map/triangular_solve/custom-call.0 | solution.py:82
  308.7 5.3 fusion.3
  315.2 6.7 %all-gather.2 = f32[128,128]{1,0:T(8,128)S(1)} all-gather(f32[32,128]{1,0:T(8,128)S(1)} %slice.173), channel_id=4, replica_groups=mesh['grp'=16,'row'=8,'col'=4] {'col'}, dimensions={0}, use_global_device_ids=true | all-gather | bytes 81920 | tf_op jit(solution)/shard_map/all_gather | solution.py:23
  322.0 19.7 %all_to_all.38 = f32[16,32,128]{2,1,0:T(8,128)S(1)} all-to-all(f32[16,32,128]{2,1,0:T(8,128)S(1)} %broadcast_in_dim.117), channel_id=1, replica_groups=mesh['grp'=16,'row'=8,'col'=4] {'grp'}, dimensions={0} | all-to-all | bytes 524288 | tf_op jit(solution)/shard_map/all_to_all | solution.py:34
  343.7 37.1 %all-gather.18.cloned.1.call-done = f32[4096,128]{0,1:T(8,128)} async-done(((f32[512,128]{0,1:T(8,128)}), f32[4096,128]{0,1:T(8,128)}) %all-gather.18.cloned.1.call-update) | async-done | bytes 2097168 | tf_op jit(solution)/shard_map/all_gather | solution.py:80
  381.7 0.9 fusion.24
  382.6 11.7 %cholesky.111 = f32[128,128]{1,0:T(8,128)S(1)} custom-call(f32[128,128]{1,0:T(8,128)S(1)} %fusion.24), custom_call_target="Cholesky" | custom-call | tf_op jit(solution)/shard_map/jit(cholesky)/cholesky | solution.py:81
  395.7 9.8 %custom-call.11 = f32[1,128,128]{1,2,0:T(8,128)S(1)} custom-call(f32[1,128,128]{2,1,0:T(8,128)S(1)} %fusion.16), custom_call_target="InvertDiagBlocksLowerTriangular" | custom-call | tf_op jit(solution)/shard_map/triangular_solve/custom-call.0 | solution.py:82
  405.5 5.3 fusion.2
  412.0 6.7 %all-gather.3 = f32[128,128]{1,0:T(8,128)S(1)} all-gather(f32[32,128]{1,0:T(8,128)S(1)} %slice.177), channel_id=5, replica_groups=mesh['grp'=16,'row'=8,'col'=4] {'col'}, dimensions={0}, use_global_device_ids=true | all-gather | bytes 81920 | tf_op jit(solution)/shard_map/all_gather | solution.py:23
  418.8 19.7 %all_to_all.39 = f32[16,32,128]{2,1,0:T(8,128)S(1)} all-to-all(f32[16,32,128]{2,1,0:T(8,128)S(1)} %broadcast_in_dim.120), channel_id=1, replica_groups=mesh['grp'=16,'row'=8,'col'=4] {'grp'}, dimensions={0} | all-to-all | bytes 524288 | tf_op jit(solution)/shard_map/all_to_all | solution.py:34
  440.2 37.4 %all-gather.20.cloned.1.call-done = f32[4096,128]{0,1:T(8,128)} async-done(((f32[512,128]{0,1:T(8,128)}), f32[4096,128]{0,1:T(8,128)}) %all-gather.20.cloned.1.call-update) | async-done | bytes 2097168 | tf_op jit(solution)/shard_map/all_gather | solution.py:80
  478.6 0.9 fusion.22
  479.4 11.7 %cholesky.122 = f32[128,128]{1,0:T(8,128)S(1)} custom-call(f32[128,128]{1,0:T(8,128)S(1)} %fusion.22), custom_call_target="Cholesky" | custom-call | tf_op jit(solution)/shard_map/jit(cholesky)/cholesky | solution.py:81
  492.5 9.8 %custom-call.12 = f32[1,128,128]{1,2,0:T(8,128)S(1)} custom-call(f32[1,128,128]{2,1,0:T(8,128)S(1)} %fusion.17), custom_call_target="InvertDiagBlocksLowerTriangular" | custom-call | tf_op jit(solution)/shard_map/triangular_solve/custom-call.0 | solution.py:82
  502.3 5.3 fusion.1
  508.8 6.7 %all-gather.4 = f32[128,128]{1,0:T(8,128)S(1)} all-gather(f32[32,128]{1,0:T(8,128)S(1)} %slice.181), channel_id=6, replica_groups=mesh['grp'=16,'row'=8,'col'=4] {'col'}, dimensions={0}, use_global_device_ids=true | all-gather | bytes 81920 | tf_op jit(solution)/shard_map/all_gather | solution.py:23
  515.6 19.9 %all_to_all.40 = f32[16,32,128]{2,1,0:T(8,128)S(1)} all-to-all(f32[16,32,128]{2,1,0:T(8,128)S(1)} %broadcast_in_dim.123), channel_id=1, replica_groups=mesh['grp'=16,'row'=8,'col'=4] {'grp'}, dimensions={0} | all-to-all | bytes 524288 | tf_op jit(solution)/shard_map/all_to_all | solution.py:34
  537.0 37.6 %all-gather.22.cloned.1.call-done = f32[4096,128]{0,1:T(8,128)} async-done(((f32[512,128]{0,1:T(8,128)}), f32[4096,128]{0,1:T(8,128)}) %all-gather.22.cloned.1.call-update) | async-done | bytes 2097168 | tf_op jit(solution)/shard_map/all_gather | solution.py:80
  575.6 0.9 fusion.20
  576.5 11.7 %cholesky.133 = f32[128,128]{1,0:T(8,128)S(1)} custom-call(f32[128,128]{1,0:T(8,128)S(1)} %fusion.20), custom_call_target="Cholesky" | custom-call | tf_op jit(solution)/shard_map/jit(cholesky)/cholesky | solution.py:81
  589.5 9.8 %custom-call.13 = f32[1,128,128]{1,2,0:T(8,128)S(1)} custom-call(f32[1,128,128]{2,1,0:T(8,128)S(1)} %fusion.18), custom_call_target="InvertDiagBlocksLowerTriangular" | custom-call | tf_op jit(solution)/shard_map/triangular_solve/custom-call.0 | solution.py:82
  599.3 5.3 fusion
  606.1 54.1 %all_to_all.41 = f32[16,32,1024]{2,1,0:T(8,128)S(1)} all-to-all(f32[16,32,1024]{2,1,0:T(8,128)S(1)} %broadcast_in_dim.125), channel_id=1, replica_groups=mesh['grp'=16,'row'=8,'col'=4] {'grp'}, dimensions={0} | all-to-all | bytes 4194304 | tf_op jit(solution)/shard_map/all_to_all | solution.py:34
  660.2 1.3 copy.102
  (89 shorter events, 27.2 us)
Async XLA Ops:
  6.5 51.5 %all-gather.12.cloned.1.call-start = ((), (), s32[]{:S(2)}) async-start(), calls=%async_computation.7 | async-start | bytes 2359296 | tf_op jit(solution)/shard_map/all_gather | solution.py:51
  7.3 180.1 %all-gather.14.cloned.1.call-start = ((), (), s32[]{:S(2)}) async-start(), calls=%async_computation.8 | async-start | bytes 2359296 | tf_op jit(solution)/shard_map/all_gather | solution.py:80
  7.3 3.4 copy-start.1
  7.3 3.8 copy-start
  150.0 134.0 %all-gather.16.cloned.1.call-start = ((), (), s32[]{:S(2)}) async-start(), calls=%async_computation.9 | async-start | bytes 2359296 | tf_op jit(solution)/shard_map/all_gather | solution.py:80
  245.7 135.1 %all-gather.18.cloned.1.call-start = ((), (), s32[]{:S(2)}) async-start(), calls=%async_computation.10 | async-start | bytes 2359296 | tf_op jit(solution)/shard_map/all_gather | solution.py:80
  342.6 135.1 %all-gather.20.cloned.1.call-start = ((), (), s32[]{:S(2)}) async-start(), calls=%async_computation.11 | async-start | bytes 2359296 | tf_op jit(solution)/shard_map/all_gather | solution.py:80
  439.4 135.3 %all-gather.22.cloned.1.call-start = ((), (), s32[]{:S(2)}) async-start(), calls=%async_computation.12 | async-start | bytes 2359296 | tf_op jit(solution)/shard_map/all_gather | solution.py:80
Sparse Core Ops, SparseCore 0:
  9.4 48.5 all-gather.11
  150.1 37.1 all-gather.13
  245.9 38.0 all-gather.15
  342.7 38.0 all-gather.17
  439.5 38.0 all-gather.19
  536.5 38.1 all-gather.21
where the time goes:
time: 675 us; the launch traced here: 669 us
  blocking collectives  237 us (35%)
  waiting for transfers between devices  230 us (34%)
  other arithmetic  127 us (19%)
  matrix products  37.3 us (6%)
  local copies, waits for them, and re-layouts  22.1 us (3%)
  between operations  14.2 us (2%)
    all_gather x5, waiting for transfers between devices, on_device(): column = lax.all_gather(panel_piece, 'row', axis=0, tiled=True)  186 us
    all_to_all x6, blocking collectives, sent_to_all(): lax.all_to_all(jnp.broadcast_to(shard[None], (length, *shard.shape)), axi...  149 us
    another operation x15, other arithmetic, on_device(): factor_block = jnp.linalg.cholesky(column[offset:offset + BLK])  61.9 us
    all_to_all x1, blocking collectives, sum_at_owner(): lax.all_to_all(parts, axis, split_axis=0, concat_axis=0, tiled=True)  54.1 us
    another operation x10, other arithmetic, on_device(): lax.linalg.triangular_solve(factor_block, column, left_side=False, lower=...  52.3 us
    all_gather x1, waiting for transfers between devices, on_device(): every_block = lax.all_gather(transforms, 'row', axis=1, tiled=True)[0]  43.2 us
    all_gather x5, blocking collectives, from_root(): lax.all_gather(shard, axis)  33.7 us
    another operation x5, matrix products, on_device(): lax.linalg.triangular_solve(factor_block, column, left_side=False, lower=...  26.2 us
  transfers between devices with their start and end apart: 6, of which 6 were waited for; matrix products, arithmetic and copies ran while one was open for 2% of the time, Pallas kernels for 0%

commit v1 on v0

--- a/solution.py
+++ b/solution.py
@@ -77,7 +77,11 @@
         inside = offset - holder * width
         panel_piece = from_root(matrix[:, inside : inside + BLK], "col", holder)
         panel_piece = gather_directly(panel_piece, "grp", 0)
-        column = lax.all_gather(panel_piece, "row", axis=0, tiled=True)
+        size = lax.axis_size("row")
+        repeats = [size if d == 0 else 1 for d in range(panel_piece.ndim)]
+        column = lax.all_to_all(
+            jnp.tile(panel_piece, repeats), "row", split_axis=0, concat_axis=0, tiled=True
+        )
         factor_block = jnp.linalg.cholesky(column[offset : offset + BLK])
         factor = lax.linalg.triangular_solve(
             factor_block, column, left_side=False, lower=True, transpose_a=True

time: 675 us -> 747 us (1.11)
  waiting for transfers between devices: 230 us -> 292 us
  starting transfers between devices: 1.17 us -> 19.7 us
  local copies, waits for them, and re-layouts: 22.1 us -> 38 us
  blocking collectives: 237 us -> 222 us
    all_to_all x0 -> x5, waiting for transfers between devices: none -> 248 us  [on_device(): lax.all_to_all(jnp.tile(panel_piece, repeats), 'row', split_axis=0, conca...]
    all_gather x5 -> x0, waiting for transfers between devices: 186 us -> none  [on_device(): column = lax.all_gather(panel_piece, 'row', axis=0, tiled=True)]
    all_to_all x0 -> x5, starting transfers between devices: none -> 19.7 us  [on_device(): lax.all_to_all(jnp.tile(panel_piece, repeats), 'row', split_axis=0, conca...]
    all_to_all x6, blocking collectives: 149 us -> 134 us  [sent_to_all(): lax.all_to_all(jnp.broadcast_to(shard[None], (length, *shard.shape)), axi...]
    all_to_all x0 -> x5, local copies, waits for them, and re-layouts: none -> 9.11 us  [on_device(): lax.all_to_all(jnp.tile(panel_piece, repeats), 'row', split_axis=0, conca...]
    another operation x0 -> x10, local copies, waits for them, and re-layouts: none -> 8.56 us  [on_device(): jnp.tile(panel_piece, repeats)]
where the time goes in v1:
time: 747 us; the launch traced here: 740 us
  waiting for transfers between devices  292 us (39%)
  blocking collectives  222 us (30%)
  other arithmetic  124 us (17%)
  local copies, waits for them, and re-layouts  38 us (5%)
  matrix products  30.8 us (4%)
  starting transfers between devices  19.7 us (3%)
  between operations  14.5 us (2%)
    all_to_all x5, waiting for transfers between devices, on_device(): lax.all_to_all(jnp.tile(panel_piece, repeats), 'row', split_axis=0, conca...  248 us
    all_to_all x6, blocking collectives, sent_to_all(): lax.all_to_all(jnp.broadcast_to(shard[None], (length, *shard.shape)), axi...  134 us
    another operation x15, other arithmetic, on_device(): factor_block = jnp.linalg.cholesky(column[offset:offset + BLK])  61.9 us
    all_to_all x1, blocking collectives, sum_at_owner(): lax.all_to_all(parts, axis, split_axis=0, concat_axis=0, tiled=True)  54.1 us
    another operation x10, other arithmetic, on_device(): lax.linalg.triangular_solve(factor_block, column, left_side=False, lower=...  52.3 us
    all_gather x1, waiting for transfers between devices, on_device(): every_block = lax.all_gather(transforms, 'row', axis=1, tiled=True)[0]  43.2 us
    all_gather x5, blocking collectives, from_root(): lax.all_gather(shard, axis)  33.7 us
    another operation x5, matrix products, on_device(): lax.linalg.triangular_solve(factor_block, column, left_side=False, lower=...  19.7 us
  transfers between devices with their start and end apart: 6, of which 6 were waited for; matrix products, arithmetic and copies ran while one was open for 2% of the time, Pallas kernels for 0%

profile of v1, /device:TPU:4, one launch (start us, length us, event | category | flops | bytes accessed | tf_op | source)
XLA Modules:
  0.0 740.1 jit_solution(13373262915643850274)
XLA Ops:
  7.3 3.4 copy.108
  11.1 3.7 fusion.4
  14.8 43.2 %all-gather.7.cloned.1.call-done = f32[1,32,128,128]{3,2,0,1:T(8,128)} async-done(((f32[1,4,128,128]{3,2,0,1:T(8,128)}), f32[1,32,128,128]{3,2,0,1:T(8,128)}) %all-gather.7.cloned.1.call-update) | async-done | bytes 2097168 | tf_op jit(solution)/shard_map/all_gather | solution.py:51
  58.0 4.3 convolution_bitcast_fusion.5
  62.3 2.3 gather_fusion
  66.2 2.3 gather_fusion.1
  72.3 54.1 %all_to_all.80 = f32[16,32,1024]{2,1,0:T(8,128)S(1)} all-to-all(f32[16,32,1024]{2,1,0:T(8,128)S(1)} %broadcast_select_fusion), channel_id=1, replica_groups=mesh['grp'=16,'row'=8,'col'=4] {'grp'}, dimensions={0} | all-to-all | bytes 4194304 | tf_op jit(solution)/shard_map/all_to_all | solution.py:18
  126.5 6.7 all-gather
  133.3 15.9 %all_to_all.81 = f32[16,32,128]{2,1,0:T(8,128)S(1)} all-to-all(f32[16,32,128]{2,1,0:T(8,128)S(1)} %broadcast_in_dim.111), channel_id=1, replica_groups=mesh['grp'=16,'row'=8,'col'=4] {'grp'}, dimensions={0} | all-to-all | bytes 524288 | tf_op jit(solution)/shard_map/all_to_all | solution.py:34
  150.8 4.2 all-to-all-start.2
  155.8 49.0 %all-to-all-done.2 = f32[8,512,128]{1,2,0:T(8,128)S(1)} async-done(((f32[8,512,128]{1,2,0:T(8,128)}), f32[8,512,128]{1,2,0:T(8,128)S(1)}, u32[]{:S(2)}, u32[]{:S(2)}) %all-to-all-start.2) | async-done | bytes 2097184 | tf_op jit(solution)/shard_map/all_to_all | solution.py:82
  206.1 1.8 copy.103
  208.1 11.7 %cholesky.89 = f32[128,128]{1,0:T(8,128)S(1)} custom-call(f32[128,128]{1,0:T(8,128)S(1)} %fusion.28), custom_call_target="Cholesky" | custom-call | tf_op jit(solution)/shard_map/jit(cholesky)/cholesky | solution.py:85
  221.1 9.8 %custom-call.9 = f32[1,128,128]{1,2,0:T(8,128)S(1)} custom-call(f32[1,128,128]{2,1,0:T(8,128)S(1)} %fusion.14), custom_call_target="InvertDiagBlocksLowerTriangular" | custom-call | tf_op jit(solution)/shard_map/triangular_solve/custom-call.0 | solution.py:86
  230.9 3.5 convolution_bitcast_fusion.4
  235.8 6.7 all-gather.1
  242.6 16.0 %all_to_all.82 = f32[16,32,128]{2,1,0:T(8,128)S(1)} all-to-all(f32[16,32,128]{2,1,0:T(8,128)S(1)} %broadcast_in_dim.114), channel_id=1, replica_groups=mesh['grp'=16,'row'=8,'col'=4] {'grp'}, dimensions={0} | all-to-all | bytes 524288 | tf_op jit(solution)/shard_map/all_to_all | solution.py:34
  260.3 4.0 all-to-all-start.4
  265.0 49.8 %all-to-all-done.4 = f32[8,512,128]{1,2,0:T(8,128)S(1)} async-done(((f32[8,512,128]{1,2,0:T(8,128)}), f32[8,512,128]{1,2,0:T(8,128)S(1)}, u32[]{:S(2)}, u32[]{:S(2)}) %all-to-all-start.4) | async-done | bytes 2097184 | tf_op jit(solution)/shard_map/all_to_all | solution.py:82
  316.1 1.8 copy.104
  318.1 11.7 %cholesky.100 = f32[128,128]{1,0:T(8,128)S(1)} custom-call(f32[128,128]{1,0:T(8,128)S(1)} %fusion.26), custom_call_target="Cholesky" | custom-call | tf_op jit(solution)/shard_map/jit(cholesky)/cholesky | solution.py:85
  331.1 9.8 %custom-call.10 = f32[1,128,128]{1,2,0:T(8,128)S(1)} custom-call(f32[1,128,128]{2,1,0:T(8,128)S(1)} %fusion.15), custom_call_target="InvertDiagBlocksLowerTriangular" | custom-call | tf_op jit(solution)/shard_map/triangular_solve/custom-call.0 | solution.py:86
  340.9 4.1 fusion.3
  346.3 6.7 all-gather.2
  353.1 15.7 %all_to_all.83 = f32[16,32,128]{2,1,0:T(8,128)S(1)} all-to-all(f32[16,32,128]{2,1,0:T(8,128)S(1)} %broadcast_in_dim.117), channel_id=1, replica_groups=mesh['grp'=16,'row'=8,'col'=4] {'grp'}, dimensions={0} | all-to-all | bytes 524288 | tf_op jit(solution)/shard_map/all_to_all | solution.py:34
  370.5 3.8 all-to-all-start.6
  375.1 49.8 %all-to-all-done.6 = f32[8,512,128]{1,2,0:T(8,128)S(1)} async-done(((f32[8,512,128]{1,2,0:T(8,128)}), f32[8,512,128]{1,2,0:T(8,128)S(1)}, u32[]{:S(2)}, u32[]{:S(2)}) %all-to-all-start.6) | async-done | bytes 2097184 | tf_op jit(solution)/shard_map/all_to_all | solution.py:82
  426.1 1.8 copy.105
  428.1 11.7 %cholesky.111 = f32[128,128]{1,0:T(8,128)S(1)} custom-call(f32[128,128]{1,0:T(8,128)S(1)} %fusion.24), custom_call_target="Cholesky" | custom-call | tf_op jit(solution)/shard_map/jit(cholesky)/cholesky | solution.py:85
  441.2 9.8 %custom-call.11 = f32[1,128,128]{1,2,0:T(8,128)S(1)} custom-call(f32[1,128,128]{2,1,0:T(8,128)S(1)} %fusion.16), custom_call_target="InvertDiagBlocksLowerTriangular" | custom-call | tf_op jit(solution)/shard_map/triangular_solve/custom-call.0 | solution.py:86
  451.0 4.1 fusion.2
  456.4 6.7 all-gather.3
  463.1 15.7 %all_to_all.84 = f32[16,32,128]{2,1,0:T(8,128)S(1)} all-to-all(f32[16,32,128]{2,1,0:T(8,128)S(1)} %broadcast_in_dim.120), channel_id=1, replica_groups=mesh['grp'=16,'row'=8,'col'=4] {'grp'}, dimensions={0} | all-to-all | bytes 524288 | tf_op jit(solution)/shard_map/all_to_all | solution.py:34
  480.6 3.8 all-to-all-start.8
  485.1 49.8 %all-to-all-done.8 = f32[8,512,128]{1,2,0:T(8,128)S(1)} async-done(((f32[8,512,128]{1,2,0:T(8,128)}), f32[8,512,128]{1,2,0:T(8,128)S(1)}, u32[]{:S(2)}, u32[]{:S(2)}) %all-to-all-start.8) | async-done | bytes 2097184 | tf_op jit(solution)/shard_map/all_to_all | solution.py:82
  536.2 1.8 copy.106
  538.2 11.7 %cholesky.122 = f32[128,128]{1,0:T(8,128)S(1)} custom-call(f32[128,128]{1,0:T(8,128)S(1)} %fusion.22), custom_call_target="Cholesky" | custom-call | tf_op jit(solution)/shard_map/jit(cholesky)/cholesky | solution.py:85
  551.2 9.8 %custom-call.12 = f32[1,128,128]{1,2,0:T(8,128)S(1)} custom-call(f32[1,128,128]{2,1,0:T(8,128)S(1)} %fusion.17), custom_call_target="InvertDiagBlocksLowerTriangular" | custom-call | tf_op jit(solution)/shard_map/triangular_solve/custom-call.0 | solution.py:86
  561.1 4.1 fusion.1
  566.4 6.7 all-gather.4
  573.2 15.7 %all_to_all.85 = f32[16,32,128]{2,1,0:T(8,128)S(1)} all-to-all(f32[16,32,128]{2,1,0:T(8,128)S(1)} %broadcast_in_dim.123), channel_id=1, replica_groups=mesh['grp'=16,'row'=8,'col'=4] {'grp'}, dimensions={0} | all-to-all | bytes 524288 | tf_op jit(solution)/shard_map/all_to_all | solution.py:34
  590.7 3.9 all-to-all-start.10
  595.3 49.8 %all-to-all-done.10 = f32[8,512,128]{1,2,0:T(8,128)S(1)} async-done(((f32[8,512,128]{1,2,0:T(8,128)}), f32[8,512,128]{1,2,0:T(8,128)S(1)}, u32[]{:S(2)}, u32[]{:S(2)}) %all-to-all-start.10) | async-done | bytes 2097184 | tf_op jit(solution)/shard_map/all_to_all | solution.py:82
  646.3 1.8 copy.107
  648.3 11.7 %cholesky.133 = f32[128,128]{1,0:T(8,128)S(1)} custom-call(f32[128,128]{1,0:T(8,128)S(1)} %fusion.20), custom_call_target="Cholesky" | custom-call | tf_op jit(solution)/shard_map/jit(cholesky)/cholesky | solution.py:85
  661.4 9.8 %custom-call.13 = f32[1,128,128]{1,2,0:T(8,128)S(1)} custom-call(f32[1,128,128]{2,1,0:T(8,128)S(1)} %fusion.18), custom_call_target="InvertDiagBlocksLowerTriangular" | custom-call | tf_op jit(solution)/shard_map/triangular_solve/custom-call.0 | solution.py:86
  671.2 4.1 fusion
  676.8 54.7 %all_to_all.86 = f32[16,32,1024]{2,1,0:T(8,128)S(1)} all-to-all(f32[16,32,1024]{2,1,0:T(8,128)S(1)} %broadcast_in_dim.125), channel_id=1, replica_groups=mesh['grp'=16,'row'=8,'col'=4] {'grp'}, dimensions={0} | all-to-all | bytes 4194304 | tf_op jit(solution)/shard_map/all_to_all | solution.py:34
  (104 shorter events, 40.8 us)
Async XLA Ops:
  6.5 51.5 %all-gather.7.cloned.1.call-start = ((), (), s32[]{:S(2)}) async-start(), calls=%async_computation.12 | async-start | bytes 2359296 | tf_op jit(solution)/shard_map/all_gather | solution.py:51
  7.3 3.4 copy-start.6
  7.3 3.8 copy-start.5
  150.8 53.9 %all-to-all-start.2 = ((f32[8,512,128]{1,2,0:T(8,128)}), f32[8,512,128]{1,2,0:T(8,128)S(1)}, u32[]{:S(2)}, u32[]{:S(2)}) async-start(f32[8,512,128]{1,2,0:T(8,128)} %tile.41), calls=%async_computation.2 | async-start | bytes 4194304 | tf_op jit(solution)/shard_map/all_to_all | solution.py:82
  204.8 1.3 copy-start
  260.3 54.5 %all-to-all-start.4 = ((f32[8,512,128]{1,2,0:T(8,128)}), f32[8,512,128]{1,2,0:T(8,128)S(1)}, u32[]{:S(2)}, u32[]{:S(2)}) async-start(f32[8,512,128]{1,2,0:T(8,128)} %tile.43), calls=%async_computation.4 | async-start | bytes 4194304 | tf_op jit(solution)/shard_map/all_to_all | solution.py:82
  314.8 1.3 copy-start.1
  370.5 54.3 %all-to-all-start.6 = ((f32[8,512,128]{1,2,0:T(8,128)}), f32[8,512,128]{1,2,0:T(8,128)S(1)}, u32[]{:S(2)}, u32[]{:S(2)}) async-start(f32[8,512,128]{1,2,0:T(8,128)} %tile.45), calls=%async_computation.6 | async-start | bytes 4194304 | tf_op jit(solution)/shard_map/all_to_all | solution.py:82
  424.8 1.3 copy-start.2
  480.6 54.3 %all-to-all-start.8 = ((f32[8,512,128]{1,2,0:T(8,128)}), f32[8,512,128]{1,2,0:T(8,128)S(1)}, u32[]{:S(2)}, u32[]{:S(2)}) async-start(f32[8,512,128]{1,2,0:T(8,128)} %tile.47), calls=%async_computation.8 | async-start | bytes 4194304 | tf_op jit(solution)/shard_map/all_to_all | solution.py:82
  534.9 1.3 copy-start.3
  590.7 54.3 %all-to-all-start.10 = ((f32[8,512,128]{1,2,0:T(8,128)}), f32[8,512,128]{1,2,0:T(8,128)S(1)}, u32[]{:S(2)}, u32[]{:S(2)}) async-start(f32[8,512,128]{1,2,0:T(8,128)} %tile.49), calls=%async_computation.10 | async-start | bytes 4194304 | tf_op jit(solution)/shard_map/all_to_all | solution.py:82
  645.0 1.3 copy-start.4
Sparse Core Ops, SparseCore 0:
  9.4 48.5 all-gather.6
